TPU v7x, 32 devices: a whole 2x2x4 slice. The times are simulated.
32 devices in a mesh: wide: 8 (over z, x), narrow: 4 (over y, core).
Axes of the slice: x: 2, y: 2, z: 4, core: 2. Of those that a mesh axis runs over, the one named last changes fastest.
Arguments:
- raw_features: bfloat16 [10240, 100], P('wide'), may hold values from -60 to 60
- placement: int32 [10240], P('wide'), may hold values from 0 to 10239, as said below
- query_counts: int32 [8], replicated, may hold values from 1 to 1024, 2048 in all
- out_grad: bfloat16 [8, 2048, 768], P('wide', 'narrow'), may hold values from -6 to 6
- w_emb: bfloat16 [100, 768], replicated, may hold values from -0.625 to 0.625
- b_emb: float32 [768], replicated, may hold values from -1.5 to 1.5
- ln1_gain: float32 [768], replicated, may hold values from 0.5 to 1.5
- ln1_bias: float32 [768], replicated, may hold values from -1.5 to 1.5
- w_qkv: bfloat16 [3, 768, 768], P(None, None, 'narrow'), may hold values from -0.21875 to 0.21875
- w_out: bfloat16 [768, 768], P('narrow'), may hold values from -3.5 to 3.5
- ln2_gain: float32 [768], replicated, may hold values from 0.5 to 1.5
- ln2_bias: float32 [768], replicated, may hold values from -1.5 to 1.5
- w_fc1: bfloat16 [768, 3072], P(None, 'narrow'), may hold values from -0.21875 to 0.21875
- b_fc1: float32 [3072], P('narrow'), may hold values from -2.5 to 2.5
- w_fc2: bfloat16 [3072, 768], P('narrow'), may hold values from -0.109375 to 0.109375
Outputs:
- layer_out: bfloat16 [8, 2048, 768], P('wide', 'narrow')
- raw_grad: float32 [10240, 100], P('wide')
- w_emb_grad: float32 [100, 768], replicated
- b_emb_grad: float32 [768], replicated
- ln1_gain_grad: float32 [768], replicated
- ln1_bias_grad: float32 [768], replicated
- w_qkv_grad: float32 [3, 768, 768], P(None, None, 'narrow')
- w_out_grad: float32 [768, 768], P('narrow')
- ln2_gain_grad: float32 [768], replicated
- ln2_bias_grad: float32 [768], replicated
- w_fc1_grad: float32 [768, 3072], P(None, 'narrow')
- b_fc1_grad: float32 [3072], P('narrow')
- w_fc2_grad: float32 [3072, 768], P('narrow')
Inputs may be any that keep to these rules, and one draw needn't show every extreme that they name: `placement`: arriving row block s (rows s * 1280 to (s + 1) * 1280 - 1) holds exactly the logical rows congruent to s modulo 8, in a random order; each logical row arrives once. `query_counts`: the counts sum to 2048; the largest is exactly 1024.
All inputs are finite; a program needn't handle non-finite values.
Results may differ from a plain program's by a relative error of at most 0.0109.
Values may be sent and summed in bfloat16 or wider, within the bound.
A program may use at most 128 MiB of HBM per device.

v0:
```python
import jax
import jax.numpy as jnp
from jax import lax
from jax.sharding import PartitionSpec as P

HD = 64
CTX = 1024


EPS = 1e-05
HIGHEST = lax.Precision.HIGHEST


def norm_apply(values, gain, bias):
    centre = values - jnp.mean(values, -1, keepdims=True)
    spread = jnp.mean(centre * centre, -1, keepdims=True)
    return centre * lax.rsqrt(spread + EPS) * gain + bias


def gelu_exact(values):
    return 0.5 * values * (1.0 + jax.scipy.special.erf(values * 0.7071067811865476))


def plain_dot(left, right):
    return jnp.dot(left, right, preferred_element_type=jnp.float32)


def rows_dot(left, right):
    return lax.dot_general(
        left, right, (((0,), (0,)), ((), ())), preferred_element_type=jnp.float32
    )


def rows_dot_exact(left, right):
    return lax.dot_general(
        left, right, (((0,), (0,)), ((), ())), precision=HIGHEST, preferred_element_type=jnp.float32
    )


def trans_dot(left, right):
    return lax.dot_general(
        left, right, (((1,), (1,)), ((), ())), preferred_element_type=jnp.float32
    )


def route_rows(placement, query_counts, wide_count, slot_count):
    table_count = query_counts.shape[0]
    starts = (
        jnp.arange(table_count, dtype=jnp.int32) * CTX + jnp.cumsum(query_counts) - query_counts
    )
    table_id = jnp.sum((placement[:, None] >= starts[None, :]).astype(jnp.int32), 1) - 1
    member = table_id[:, None] == jnp.arange(table_count, dtype=jnp.int32)[None, :]
    local_index = placement - jnp.sum(jnp.where(member, starts[None, :], 0), 1)
    dest_slot = table_id * slot_count + local_index // wide_count
    return (starts, member, local_index, dest_slot)


def to_table(received, roll_shift):
    rolled = jnp.roll(received, -roll_shift, axis=0)
    return jnp.transpose(rolled, (1, 0, 2)).reshape(-1, received.shape[2])


def to_sources(table_rows, roll_shift, wide_count):
    slot_count = table_rows.shape[0] // wide_count
    split_rows = table_rows.reshape(slot_count, wide_count, table_rows.shape[1])
    return jnp.roll(jnp.transpose(split_rows, (1, 0, 2)), roll_shift, axis=0)


def attend_forward(queries, keys_ctx, values_ctx, block_rows):
    head_count = queries.shape[1] // HD
    score_scale = HD ** (-0.5)
    key_heads = keys_ctx.reshape(-1, head_count, HD)
    value_heads = values_ctx.reshape(-1, head_count, HD)

    def attend(query_block):
        scores = (
            jnp.einsum("qhd,khd->hqk", query_block, key_heads, preferred_element_type=jnp.float32)
            * score_scale
        )
        row_max = jnp.max(scores, -1, keepdims=True)
        exp_scores = jnp.exp(scores - row_max)
        row_total = jnp.sum(exp_scores, -1, keepdims=True)
        attn_probs = (exp_scores / row_total).astype(jnp.bfloat16)
        mixed = jnp.einsum(
            "hqk,khd->qhd", attn_probs, value_heads, preferred_element_type=jnp.float32
        )
        return (mixed.astype(jnp.bfloat16), (row_max + jnp.log(row_total))[..., 0])

    blocks = queries.reshape(-1, block_rows, head_count, HD)
    mixed, log_total = lax.map(attend, blocks)
    return (mixed.reshape(queries.shape[0], -1), log_total)


def attend_backward(queries, keys_ctx, values_ctx, mixed_grad, log_total, block_rows):
    head_count = queries.shape[1] // HD
    score_scale = HD ** (-0.5)
    key_heads = keys_ctx.reshape(-1, head_count, HD)
    value_heads = values_ctx.reshape(-1, head_count, HD)

    def step_block(carried, inputs):
        key_grad, value_grad = carried
        query_block, grad_block, log_block = inputs
        scores = (
            jnp.einsum("qhd,khd->hqk", query_block, key_heads, preferred_element_type=jnp.float32)
            * score_scale
        )
        attn_probs = jnp.exp(scores - log_block[..., None])
        probs_low = attn_probs.astype(jnp.bfloat16)
        probs_grad = jnp.einsum(
            "qhd,khd->hqk", grad_block, value_heads, preferred_element_type=jnp.float32
        )
        value_grad = value_grad + jnp.einsum(
            "hqk,qhd->khd", probs_low, grad_block, preferred_element_type=jnp.float32
        )
        row_inner = jnp.sum(attn_probs * probs_grad, -1, keepdims=True)
        score_grad = (attn_probs * (probs_grad - row_inner)).astype(jnp.bfloat16)
        query_grad = (
            jnp.einsum("hqk,khd->qhd", score_grad, key_heads, preferred_element_type=jnp.float32)
            * score_scale
        )
        key_grad = (
            key_grad
            + jnp.einsum(
                "hqk,qhd->khd", score_grad, query_block, preferred_element_type=jnp.float32
            )
            * score_scale
        )
        return ((key_grad, value_grad), query_grad)

    query_blocks = queries.reshape(-1, block_rows, head_count, HD)
    grad_blocks = mixed_grad.reshape(-1, block_rows, head_count, HD)
    zero_keys = jnp.zeros((keys_ctx.shape[0], head_count, HD), jnp.float32)
    (key_grad, value_grad), query_grad = lax.scan(
        step_block, (zero_keys, zero_keys), (query_blocks, grad_blocks, log_total)
    )
    context_rows = keys_ctx.shape[0]
    return (
        query_grad.reshape(queries.shape[0], -1).astype(jnp.bfloat16),
        key_grad.reshape(context_rows, -1).astype(jnp.bfloat16),
        value_grad.reshape(context_rows, -1).astype(jnp.bfloat16),
    )


def shards(
    raw_features,
    placement,
    query_counts,
    out_grad,
    w_emb,
    b_emb,
    ln1_gain,
    ln1_bias,
    w_qkv,
    w_out,
    ln2_gain,
    ln2_bias,
    w_fc1,
    b_fc1,
    w_fc2,
):
    wide_count = lax.axis_size("wide")
    wide_index = lax.axis_index("wide")
    narrow_index = lax.axis_index("narrow")
    share_rows = out_grad.shape[1]
    capacity = share_rows * lax.axis_size("narrow")
    slot_count = capacity // wide_count
    model_width = w_emb.shape[1]
    block_rows = min(512, capacity)
    starts, member, local_index, dest_slot = route_rows(
        placement, query_counts, wide_count, slot_count
    )
    roll_shift = jnp.remainder(starts[wide_index], wide_count)
    valid_rows = jnp.arange(capacity, dtype=jnp.int32) < CTX + query_counts[wide_index]
    share_start = narrow_index * share_rows
    valid_share = lax.dynamic_slice_in_dim(valid_rows, share_start, share_rows, 0)
    source_rows = raw_features.astype(jnp.float32)
    one_hot = member.astype(jnp.float32)
    context_flag = (local_index < CTX).astype(jnp.float32)
    context_hot = one_hot * context_flag[:, None]
    moments = jnp.stack(
        [
            rows_dot_exact(context_hot, source_rows),
            rows_dot_exact(context_hot, source_rows * source_rows),
        ]
    )
    moments = lax.psum(moments, "wide")
    table_mean = moments[0] / CTX
    table_var = moments[1] / CTX - table_mean * table_mean
    table_rstd = lax.rsqrt(table_var + EPS)
    row_mean = jnp.dot(one_hot, table_mean, precision=HIGHEST)
    row_rstd = jnp.dot(one_hot, table_rstd, precision=HIGHEST)
    standard = ((source_rows - row_mean) * row_rstd).astype(jnp.bfloat16)
    embedded_rows = plain_dot(standard, w_emb) + b_emb
    outgoing = (
        jnp.zeros((wide_count * slot_count, model_width), jnp.float32)
        .at[dest_slot]
        .set(embedded_rows)
    )
    received = lax.all_to_all(
        outgoing.reshape(wide_count, slot_count, model_width),
        "wide",
        split_axis=0,
        concat_axis=0,
        tiled=True,
    )
    embedded = to_table(received, roll_shift)
    embedded_share = lax.dynamic_slice_in_dim(embedded, share_start, share_rows, 0)
    normed_one = norm_apply(embedded, ln1_gain, ln1_bias).astype(jnp.bfloat16)
    queries = plain_dot(normed_one, w_qkv[0]).astype(jnp.bfloat16)
    keys_ctx = plain_dot(normed_one[:CTX], w_qkv[1]).astype(jnp.bfloat16)
    values_ctx = plain_dot(normed_one[:CTX], w_qkv[2]).astype(jnp.bfloat16)
    mixed_heads, log_total = attend_forward(queries, keys_ctx, values_ctx, block_rows)
    residual = embedded_share + lax.psum_scatter(
        plain_dot(mixed_heads, w_out), "narrow", scatter_dimension=0, tiled=True
    )
    normed_share, ln2_back = jax.vjp(norm_apply, residual, ln2_gain, ln2_bias)
    normed_two = lax.all_gather(normed_share.astype(jnp.bfloat16), "narrow", axis=0, tiled=True)
    gelu_out, gelu_back = jax.vjp(gelu_exact, plain_dot(normed_two, w_fc1) + b_fc1)
    activated = gelu_out.astype(jnp.bfloat16)
    final_share = residual + lax.psum_scatter(
        plain_dot(activated, w_fc2).astype(jnp.bfloat16), "narrow", scatter_dimension=0, tiled=True
    ).astype(jnp.float32)
    layer_out = jnp.where(valid_share[:, None], final_share, 0.0).astype(jnp.bfloat16)
    top_share = jnp.where(valid_share[:, None], out_grad[0].astype(jnp.float32), 0.0)
    top_full = lax.all_gather(top_share.astype(jnp.bfloat16), "narrow", axis=0, tiled=True)
    w_fc2_grad = rows_dot(activated, top_full)
    (pre_grad,) = gelu_back(trans_dot(top_full, w_fc2))
    pre_low = pre_grad.astype(jnp.bfloat16)
    b_fc1_grad = jnp.sum(pre_low.astype(jnp.float32), 0)
    w_fc1_grad = rows_dot(normed_two, pre_low)
    normed_grad = lax.psum_scatter(
        trans_dot(pre_low, w_fc1), "narrow", scatter_dimension=0, tiled=True
    )
    mid_ln_grad, ln2_gain_grad, ln2_bias_grad = ln2_back(normed_grad)
    mid_share = top_share + mid_ln_grad
    mid_full = lax.all_gather(mid_share.astype(jnp.bfloat16), "narrow", axis=0, tiled=True)
    w_out_grad = rows_dot(mixed_heads, mid_full)
    mixed_grad = trans_dot(mid_full, w_out).astype(jnp.bfloat16)
    query_grad, key_grad, value_grad = attend_backward(
        queries, keys_ctx, values_ctx, mixed_grad, log_total, block_rows
    )
    w_qkv_grad = jnp.stack(
        [
            rows_dot(normed_one, query_grad),
            rows_dot(normed_one[:CTX], key_grad),
            rows_dot(normed_one[:CTX], value_grad),
        ]
    )
    key_padded = jnp.pad(key_grad, ((0, capacity - CTX), (0, 0)))
    value_padded = jnp.pad(value_grad, ((0, capacity - CTX), (0, 0)))
    term = trans_dot(query_grad, w_qkv[0])
    term = term + trans_dot(key_padded, w_qkv[1])
    first_grad = lax.psum_scatter(
        term + trans_dot(value_padded, w_qkv[2]), "narrow", scatter_dimension=0, tiled=True
    )
    ln1_back = jax.vjp(norm_apply, embedded_share, ln1_gain, ln1_bias)[1]
    low_ln_grad, ln1_gain_grad, ln1_bias_grad = ln1_back(first_grad)
    low_share = (mid_share + low_ln_grad).astype(jnp.bfloat16)
    grad_embedded = lax.all_gather(low_share, "narrow", axis=0, tiled=True)
    returned = lax.all_to_all(
        to_sources(grad_embedded, roll_shift, wide_count),
        "wide",
        split_axis=0,
        concat_axis=0,
        tiled=True,
    )
    row_grad = returned.reshape(wide_count * slot_count, model_width)[dest_slot]
    w_emb_grad = rows_dot(standard, row_grad)
    b_emb_grad = jnp.sum(row_grad.astype(jnp.float32), 0)
    standard_grad = trans_dot(row_grad, w_emb)
    grad_sums = jnp.stack(
        [
            rows_dot_exact(one_hot, standard_grad),
            rows_dot_exact(one_hot, standard_grad * source_rows),
        ]
    )
    grad_sums = lax.psum(grad_sums, "wide")
    var_grad = (
        -0.5 * table_rstd * table_rstd * table_rstd * (grad_sums[1] - table_mean * grad_sums[0])
    )
    mean_grad = -table_rstd * grad_sums[0] - 2.0 * table_mean * var_grad
    row_mean_grad = jnp.dot(one_hot, mean_grad / CTX, precision=HIGHEST)
    row_var_grad = jnp.dot(one_hot, var_grad / CTX, precision=HIGHEST)
    raw_grad = standard_grad * row_rstd + context_flag[:, None] * (
        row_mean_grad + 2.0 * source_rows * row_var_grad
    )
    weight_sums = lax.psum(
        (w_emb_grad, b_emb_grad, w_qkv_grad, w_out_grad, w_fc1_grad, b_fc1_grad, w_fc2_grad), "wide"
    )
    norm_sums = lax.psum(
        (ln1_gain_grad, ln1_bias_grad, ln2_gain_grad, ln2_bias_grad), ("wide", "narrow")
    )
    return (
        layer_out[None],
        raw_grad,
        weight_sums[0],
        weight_sums[1],
        norm_sums[0],
        norm_sums[1],
        weight_sums[2],
        weight_sums[3],
        norm_sums[2],
        norm_sums[3],
        weight_sums[4],
        weight_sums[5],
        weight_sums[6],
    )


def solution(mesh):
    in_specs = (
        P("wide", None),
        P("wide"),
        P(),
        P("wide", "narrow", None),
        P(),
        P(),
        P(),
        P(),
        P(None, None, "narrow"),
        P("narrow", None),
        P(),
        P(),
        P(None, "narrow"),
        P("narrow"),
        P("narrow", None),
    )
    out_specs = (
        P("wide", "narrow", None),
        P("wide", None),
        P(),
        P(),
        P(),
        P(),
        P(None, None, "narrow"),
        P("narrow", None),
        P(),
        P(),
        P(None, "narrow"),
        P("narrow"),
        P("narrow", None),
    )
    return jax.shard_map(shards, mesh=mesh, in_specs=in_specs, out_specs=out_specs, check_vma=False)
```

profile of v0, /device:TPU:0, one launch (start us, length us, event | category | flops | bytes accessed | tf_op | source)
XLA Modules:
  0.0 1025.8 jit_solution(14869152431607084733)
XLA Ops:
  13.9 23.4 %psum.91 = f32[2,8,100]{2,1,0:T(8,128)S(1)} all-reduce(f32[2,8,100]{2,1,0:T(8,128)S(1)} %pad_maximum_fusion.1), channel_id=1, replica_groups=mesh['wide'=8,'narrow'=4] {'wide'}, use_global_device_ids=true, to_apply=%region_3.4 | all-reduce | flops 1600 | bytes 12800 | tf_op jit(solution)/shard_map/psum | solution.py:186
  44.1 11.6 %scatter_custom_fusion = f32[2048,768]{1,0:T(8,128)} fusion(s32[1280]{0:T(1024)S(1)} %compare_select_fusion, f32[1280,768]{1,0:T(8,128)} %convolution_add_fusion, f32[]{:T(128)} %constant.148.clone.1), kind=kCustom, calls=%fused_computation.75 | custom fusion | bytes 6291968 | tf_op jit(solution)/shard_map/scatter | solution.py:197
  63.1 132.0 %all-to-all-done = f32[8,256,768]{2,1,0:T(8,128)} async-done(((f32[8,256,768]{2,1,0:T(8,128)}), f32[8,256,768]{2,1,0:T(8,128)}, u32[]{:S(2)}, u32[]{:S(2)}) %all-to-all-start) | async-done | bytes 6291488 | tf_op jit(solution)/shard_map/all_to_all | solution.py:199
  195.1 6.2 fusion.143
  206.1 6.3 copy.87
  225.9 22.0 %while.27 = (s32[]{:T(128)}, bf16[4,512,3,64]{1,3,2,0:T(8,128)(2,1)}, f32[4,3,512]{2,1,0:T(4,128)}, bf16[4,512,3,64]{1,3,2,0:T(8,128)(2,1)S(1)}, bf16[1024,3,64]...) while((s32[]{:T(128)}, bf16[4,512,3,64]{1,3,2,0:T(8,128)(2,1)}, ...), condition=%wide.region_10.11_spmd, body=%wide.region_7.10_spmd.sunk | while | flops 416905728 | bytes 20105312 | solution.py:90
  255.4 56.5 %reduce-scatter.5.cloned.1.call-done = f32[512,768]{1,0:T(8,128)} async-done(((f32[2048,768]{1,0:T(8,128)}), f32[512,768]{1,0:T(8,128)}) %reduce-scatter.5.cloned.1.call-update) | async-done | bytes 1572880 | tf_op jit(solution)/shard_map/reduce_scatter | solution.py:213
  322.1 23.5 %all-gather.5.cloned.1.call-done = bf16[2048,768]{1,0:T(8,128)(2,1)} async-done(((bf16[512,768]{1,0:T(8,128)(2,1)}), bf16[2048,768]{1,0:T(8,128)(2,1)}) %all-gather.5.cloned.1.call-update) | async-done | bytes 3145744 | tf_op jit(solution)/shard_map/all_gather | solution.py:217
  345.6 7.4 fusion.146
  353.0 23.2 %all-gather.7.cloned.1.call-done = bf16[2048,768]{1,0:T(8,128)(2,1)} async-done(((bf16[512,768]{1,0:T(8,128)(2,1)}), bf16[2048,768]{1,0:T(8,128)(2,1)}) %all-gather.7.cloned.1.call-update) | async-done | bytes 3145744 | tf_op jit(solution)/shard_map/all_gather | solution.py:225
  376.3 9.9 convert_reduce_fusion
  392.5 6.5 convolution_convert_fusion
  399.1 52.3 %reduce-scatter.9.cloned.1.call-done = f32[512,768]{1,0:T(8,128)} async-done(((f32[2048,768]{1,0:T(8,128)}), f32[512,768]{1,0:T(8,128)}) %reduce-scatter.9.cloned.1.call-update) | async-done | bytes 1572880 | tf_op jit(solution)/shard_map/reduce_scatter | solution.py:231
  454.1 37.7 %reduce-scatter.7.cloned.1.call-done = bf16[512,768]{1,0:T(8,128)(2,1)} async-done(((bf16[2048,768]{1,0:T(8,128)(2,1)}), bf16[512,768]{1,0:T(8,128)(2,1)}) %reduce-scatter.7.cloned.1.call-update) | async-done | bytes 786448 | tf_op jit(solution)/shard_map/reduce_scatter | solution.py:220
  497.7 28.4 %all-gather.9.cloned.1.call-done = bf16[2048,768]{1,0:T(8,128)(2,1)} async-done(((bf16[512,768]{1,0:T(8,128)(2,1)}), bf16[2048,768]{1,0:T(8,128)(2,1)}) %all-gather.9.cloned.1.call-update) | async-done | bytes 3145744 | tf_op jit(solution)/shard_map/all_gather | solution.py:236
  535.3 40.4 %while.28 = (s32[]{:T(128)}, f32[1024,3,64]{0,2,1:T(8,128)S(1)}, f32[1024,3,64]{0,2,1:T(8,128)S(1)}, bf16[4,512,3,64]{1,3,2,0:T(8,128)(2,1)}, bf16[4,512,3,64]{1...) while((s32[]{:T(128)}, f32[1024,3,64]{0,2,1:T(8,128)S(1)}, ...), condition=%wide.region_20.21_spmd.clone, body=%wide.region_18.20_spmd.clone.sunk | while | flops 1026587136 | bytes 62175464 | solution.py:133
  584.3 58.3 %reduce-scatter.11.cloned.1.call-done = f32[512,768]{1,0:T(8,128)} async-done(((f32[2048,768]{1,0:T(8,128)}), f32[512,768]{1,0:T(8,128)}) %reduce-scatter.11.cloned.1.call-update) | async-done | bytes 1572880 | tf_op jit(solution)/shard_map/reduce_scatter | solution.py:253
  649.5 28.6 %all-gather.11.cloned.1.call-done = bf16[2048,768]{1,0:T(8,128)(2,1)} async-done(((bf16[512,768]{1,0:T(8,128)(2,1)}), bf16[2048,768]{1,0:T(8,128)(2,1)}) %all-gather.11.cloned.1.call-update) | async-done | bytes 3145744 | tf_op jit(solution)/shard_map/all_gather | solution.py:259
  683.4 5.6 all-to-all-start.1
  689.3 7.1 fusion.152
  707.9 52.2 %all-to-all-done.1 = bf16[8,256,768]{2,1,0:T(8,128)(2,1)S(1)} async-done(((bf16[8,256,768]{2,1,0:T(8,128)(2,1)}), bf16[8,256,768]{2,1,0:T(8,128)(2,1)S(1)}, u32[]{:S(2)}, u32[]{:S(2)}) %all-to-all-start.1) | async-done | bytes 3145760 | tf_op jit(solution)/shard_map/all_to_all | solution.py:260
  768.5 41.7 %all-reduce.2 = (f32[768]{0:T(1024)}, f32[768]{0:T(1024)}, f32[768]{0:T(1024)}, f32[768]{0:T(1024)}) all-reduce(f32[768]{0:T(1024)S(1)} %copy-done.56, f32[768]{0:T(1024)S(1)} %copy-done.57, f32[768]{0:T(1024)S(1)} %copy-done.54, f32[768]{0:T(1024)S(1)} %copy-done.55), channel_id=1, replica_groups=mesh['wide'=8,'narrow'=4] {'wide','narrow'}, use_global_device_ids=true, to_apply=%region_31.32 | all-reduce | flops 3072 | bytes 24576 | tf_op jit(solution)/shard_map/psum | solution.py:290
  812.1 40.1 %all-reduce.3 = (f32[2,8,100]{2,1,0:T(8,128)S(1)}, f32[768]{0:T(1024)}, f32[768]{0:T(1024)}) all-reduce(f32[2,8,100]{2,1,0:T(8,128)S(1)} %pad_maximum_fusion.2, f32[768]{0:T(1024)S(1)} %convert_reduce_fusion.1, f32[768]{0:T(1024)S(1)} %copy-done.62), channel_id=1, replica_groups=mesh['wide'=8,'narrow'=4] {'wide'}, use_global_device_ids=true, to_apply=%region_26.27 | all-reduce | flops 3136 | bytes 25088 | tf_op jit(solution)/shard_map/psum | solution.py:277
  854.0 156.6 %all-reduce.7.cloned.1.call-done = (f32[100,768]{1,0:T(8,128)}, f32[3,768,192]{1,2,0:T(8,128)}, f32[192,768]{1,0:T(8,128)}, f32[768,768]{1,0:T(8,128)}, f32[768,768]{1,0:T(8,128)}) async-done(((f32[100,768]{1,0:T(8,128)}, f32[3,768,192]{1,2,0:T(8,128)}, f32[192,768]{1,0:T(8,128)}, f32[768,768]{1,0:T(8,128)}, f32[768,768]{1,0:T(8,128)}), (f32[100,768]{1,0:T(8,128)}, f32[3,768,192]{1,2,0:T(8,128)}, ...) | async-done | bytes 7385104 | tf_op jit(solution)/shard_map/psum | solution.py:287
  (308 shorter events, 192.6 us)
Async XLA Ops:
  7.2 369.1 %copy-start = (bf16[768,768]{1,0:T(8,128)(2,1)S(1)}, bf16[768,768]{1,0:T(8,128)(2,1)}, u32[]{:S(2)}) copy-start(bf16[768,768]{1,0:T(8,128)(2,1)} %param.33) | copy-start | bytes 3538948
  55.8 139.4 %all-to-all-start = ((f32[8,256,768]{2,1,0:T(8,128)}), f32[8,256,768]{2,1,0:T(8,128)}, u32[]{:S(2)}, u32[]{:S(2)}) async-start(f32[8,256,768]{2,1,0:T(8,128)} %bitcast.277), calls=%async_computation | async-start | bytes 12582912 | tf_op jit(solution)/shard_map/all_to_all | solution.py:199
  60.5 251.4 %reduce-scatter.5.cloned.1.call-start = ((), (), s32[]{:S(2)}) async-start(), calls=%async_computation.6 | async-start | bytes 7864320 | tf_op jit(solution)/shard_map/reduce_scatter | solution.py:213
  253.8 91.8 %all-gather.5.cloned.1.call-start = ((), (), s32[]{:S(2)}) async-start(), calls=%async_computation.7 | async-start | bytes 3932160 | tf_op jit(solution)/shard_map/all_gather | solution.py:217
  255.4 60.3 %copy-start.47 = (f32[768]{0:T(1024)S(1)}, f32[768]{0:T(1024)}, u32[]{:S(2)}) copy-start(f32[768]{0:T(1024)} %param.29) | copy-start | bytes 9220
  316.9 59.4 %all-gather.7.cloned.1.call-start = ((), (), s32[]{:S(2)}) async-start(), calls=%async_computation.9 | async-start | bytes 3932160 | tf_op jit(solution)/shard_map/all_gather | solution.py:225
  321.6 129.8 %reduce-scatter.9.cloned.1.call-start = ((), (), s32[]{:S(2)}) async-start(), calls=%async_computation.10 | async-start | bytes 7864320 | tf_op jit(solution)/shard_map/reduce_scatter | solution.py:231
  392.4 99.3 %reduce-scatter.7.cloned.1.call-start = ((), (), s32[]{:S(2)}) async-start(), calls=%async_computation.8 | async-start | bytes 3932160 | tf_op jit(solution)/shard_map/reduce_scatter | solution.py:220
  399.0 55.0 %copy-start.52 = (f32[512]{0:T(512)S(1)}, f32[512]{0:T(512)}, u32[]{:S(2)}) copy-start(f32[512]{0:T(512)} %copy-done.51) | copy-start | bytes 6148
  399.0 92.7 %copy-start.59 = (pred[512]{0:T(512)(128)(4,1)S(1)}, pred[512]{0:T(512)(128)(4,1)}, u32[]{:S(2)}) copy-start(pred[512]{0:T(512)(128)(4,1)} %copy-done.58) | copy-start | bytes 1540
  399.1 127.0 %all-gather.9.cloned.1.call-start = ((), (), s32[]{:S(2)}) async-start(), calls=%async_computation.11 | async-start | bytes 3932160 | tf_op jit(solution)/shard_map/all_gather | solution.py:236
  497.4 145.2 %reduce-scatter.11.cloned.1.call-start = ((), (), s32[]{:S(2)}) async-start(), calls=%async_computation.12 | async-start | bytes 7864320 | tf_op jit(solution)/shard_map/reduce_scatter | solution.py:253
  583.6 59.0 %copy-start.46 = (f32[768]{0:T(1024)S(1)}, f32[768]{0:T(1024)}, u32[]{:S(2)}) copy-start(f32[768]{0:T(1024)} %param.25) | copy-start | bytes 9220
  583.6 94.4 %all-gather.11.cloned.1.call-start = ((), (), s32[]{:S(2)}) async-start(), calls=%async_computation.13 | async-start | bytes 3932160 | tf_op jit(solution)/shard_map/all_gather | solution.py:259
  683.4 76.8 %all-to-all-start.1 = ((bf16[8,256,768]{2,1,0:T(8,128)(2,1)}), bf16[8,256,768]{2,1,0:T(8,128)(2,1)S(1)}, u32[]{:S(2)}, u32[]{:S(2)}) async-start(bf16[8,256,768]{2,1,0:T(8,128)(2,1)} %fusion.42), calls=%async_computation.5 | async-start | bytes 6291456 | tf_op jit(solution)/shard_map/all_to_all | solution.py:260
  689.0 321.5 %all-reduce.7.cloned.1.call-start = ((), (), s32[]{:S(2)}) async-start(), calls=%async_computation.14 | async-start | bytes 14794752 | tf_op jit(solution)/shard_map/psum | solution.py:287
  767.8 42.4 %copy-start.4 = (bf16[1280,768]{1,0:T(8,128)(2,1)S(1)}, bf16[1280,768]{1,0:T(8,128)(2,1)}, u32[]{:S(2)}) copy-start(bf16[1280,768]{1,0:T(8,128)(2,1)} %gather_fusion) | copy-start | bytes 5898244
  767.8 42.4 %copy-start.37 = (bf16[100,768]{1,0:T(8,128)(2,1)S(1)}, bf16[100,768]{1,0:T(8,128)(2,1)}, u32[]{:S(2)}) copy-start(bf16[100,768]{1,0:T(8,128)(2,1)} %param.23) | copy-start | bytes 460804
  767.8 43.2 %copy-start.36 = (s32[1280]{0:T(1024)S(1)}, s32[1280]{0:T(1024)}, u32[]{:S(2)}) copy-start(s32[1280]{0:T(1024)} %copy-done.35) | copy-start | bytes 15364
  767.8 43.5 %copy-start.21 = (bf16[1280,100]{0,1:T(8,128)(2,1)S(1)}, bf16[1280,100]{0,1:T(8,128)(2,1)}, u32[]{:S(2)}) copy-start(bf16[1280,100]{0,1:T(8,128)(2,1)} %param.19) | copy-start | bytes 768004
  767.8 44.3 %copy-start.62 = (f32[768]{0:T(1024)S(1)}, f32[768]{0:T(1024)}, u32[]{:S(2)}) copy-start(f32[768]{0:T(1024)} %get-tuple-element.253) | copy-start | bytes 9220
  767.8 84.3 %copy-start.42 = (f32[2,8,100]{2,1,0:T(8,128)S(1)}, f32[2,8,100]{2,1,0:T(8,128)}, u32[]{:S(2)}) copy-start(f32[2,8,100]{2,1,0:T(8,128)} %copy-done.41) | copy-start | bytes 19204
  810.2 42.4 %copy-start.20 = (f32[1280,100]{0,1:T(8,128)S(1)}, f32[1280,100]{0,1:T(8,128)}, u32[]{:S(2)}) copy-start(f32[1280,100]{0,1:T(8,128)} %copy-done.19) | copy-start | bytes 1536004
  810.2 42.4 %copy-start.44 = (f32[1280]{0:T(1024)S(1)}, f32[1280]{0:T(1024)}, u32[]{:S(2)}) copy-start(f32[1280]{0:T(1024)} %copy-done.43) | copy-start | bytes 15364
  (63 other events, 318.3 us)
Sparse Core Ops, SparseCore 0:
  253.9 57.9 reduce-scatter.4
  317.1 28.5 all-gather.4
  347.7 28.4 all-gather.6
  392.6 58.8 reduce-scatter.8
  453.8 37.8 reduce-scatter.6
  497.6 28.4 all-gather.8
  583.8 58.8 reduce-scatter.10
  649.5 28.4 all-gather.10
  767.9 242.5 all-reduce.6
where the time goes:
time: 1040 us; the launch traced here: 1030 us
  waiting for transfers between devices  650 us (62%)
  matrix products  116 us (11%)
  blocking collectives  105 us (10%)
  local copies, waits for them, and re-layouts  66.8 us (6%)
  other arithmetic  58.8 us (6%)
  between operations  17.6 us (2%)
  starting transfers between devices  11.5 us (1%)
    psum x1, waiting for transfers between devices, shards(): lax.psum((w_emb_grad, b_emb_grad, w_qkv_grad, w_out_grad, w_fc1_grad, b_f...  157 us
    all_to_all x1, waiting for transfers between devices, shards(): lax.all_to_all(outgoing.reshape(wide_count, slot_count, model_width), 'wi...  132 us
    reduce_scatter x1, waiting for transfers between devices, shards(): lax.psum_scatter(term + trans_dot(value_padded, w_qkv[2]), 'narrow', scat...  58.3 us
    reduce_scatter x1, waiting for transfers between devices, shards(): lax.psum_scatter(plain_dot(mixed_heads, w_out), 'narrow', scatter_dimensi...  56.5 us
    reduce_scatter x1, waiting for transfers between devices, shards(): lax.psum_scatter(trans_dot(pre_low, w_fc1), 'narrow', scatter_dimension=0...  52.3 us
    all_to_all x1, waiting for transfers between devices, shards(): lax.all_to_all(to_sources(grad_embedded, roll_shift, wide_count), 'wide',...  52.2 us
    psum x1, blocking collectives, shards(): lax.psum((ln1_gain_grad, ln1_bias_grad, ln2_gain_grad, ln2_bias_grad), ('...  41.7 us
    psum x1, blocking collectives, shards(): grad_sums = lax.psum(grad_sums, 'wide')  40.1 us
  transfers between devices with their start and end apart: 11, of which 11 were waited for; matrix products, arithmetic and copies ran while one was open for 4% of the time, Pallas kernels for 0%

commit v1 on v0

v1 whole, which is shorter than its diff:
```python
import functools

import jax
import jax.numpy as jnp
from jax import lax
from jax.experimental import pallas as pl
from jax.experimental.pallas import tpu as pltpu
from jax.sharding import PartitionSpec as P

HD = 64
CTX = 1024
EPS = 1e-05
LANES = 128
F32 = jnp.float32
BF16 = jnp.bfloat16
SCALE = HD ** (-0.5)


def dot(left, right):
    return jnp.dot(left, right, preferred_element_type=F32)


def dot_tn(left, right):
    return lax.dot_general(left, right, (((0,), (0,)), ((), ())), preferred_element_type=F32)


def dot_nt(left, right):
    return lax.dot_general(left, right, (((1,), (1,)), ((), ())), preferred_element_type=F32)


def full(shape):
    return pl.BlockSpec(shape, lambda *_: (0,) * len(shape))


def params():
    return pltpu.CompilerParams(dimension_semantics=("arbitrary",))


def cost(flops, moved, trans=0):
    return pl.CostEstimate(flops=int(flops), bytes_accessed=int(moved), transcendentals=int(trans))


def standardize(rows, stats_ref):
    return ((rows.astype(F32) - stats_ref[0:1, :]) * stats_ref[1:2, :]).astype(BF16)


def centre_norm(values):
    centre = values - jnp.mean(values, -1, keepdims=True)
    rstd = lax.rsqrt(jnp.mean(centre * centre, -1, keepdims=True) + EPS)
    return centre * rstd, rstd


def project_kernel(
    block, rows_ref, w_emb_ref, b_emb_ref, gain_ref, bias_ref, w_ref, q_ref, k_ref, v_ref, stats_ref
):
    step = pl.program_id(0)

    @pl.when(step == 0)
    def _():
        context = rows_ref[0:CTX, :].astype(F32)
        mean = jnp.sum(context, 0, keepdims=True) / CTX
        var = jnp.sum(context * context, 0, keepdims=True) / CTX - mean * mean
        stats_ref[...] = jnp.zeros_like(stats_ref)
        stats_ref[0:1, :] = mean
        stats_ref[1:2, :] = lax.rsqrt(var + EPS)

    start = pl.multiple_of(step * block, block)
    standard = standardize(rows_ref[pl.ds(start, block), :], stats_ref)
    embedded = dot(standard, w_emb_ref[...]) + b_emb_ref[...]
    normed = (centre_norm(embedded)[0] * gain_ref[...] + bias_ref[...]).astype(BF16)
    q_ref[...] = (dot(normed, w_ref[0]).astype(BF16) * SCALE).astype(BF16)

    @pl.when(step < CTX // block)
    def _():
        k_ref[...] = dot(normed, w_ref[1]).astype(BF16)
        v_ref[...] = dot(normed, w_ref[2]).astype(BF16)


def project(rows, w_emb, b_emb, gain, bias, w_qkv):
    capacity = rows.shape[0]
    model, width = w_emb.shape[1], w_qkv.shape[2]
    block = 256
    ctx_map = lambda b: (jnp.minimum(b, CTX // block - 1), 0)
    return pl.pallas_call(
        functools.partial(project_kernel, block),
        grid=(capacity // block,),
        in_specs=[
            full((capacity, LANES)),
            full((LANES, model)),
            full((1, model)),
            full((1, model)),
            full((1, model)),
            full((3, model, width)),
        ],
        out_specs=[
            pl.BlockSpec((block, width), lambda b: (b, 0)),
            pl.BlockSpec((block, width), ctx_map),
            pl.BlockSpec((block, width), ctx_map),
            full((8, LANES)),
        ],
        out_shape=[
            jax.ShapeDtypeStruct((capacity, width), BF16),
            jax.ShapeDtypeStruct((CTX, width), BF16),
            jax.ShapeDtypeStruct((CTX, width), BF16),
            jax.ShapeDtypeStruct((8, LANES), F32),
        ],
        compiler_params=params(),
        cost_estimate=cost(2 * capacity * model * (LANES + 2 * width), 4e6),
        name="project",
    )(rows, w_emb, b_emb, gain, bias, w_qkv)


def attend_kernel(q_ref, k_ref, v_ref, mixed_ref, log_ref):
    heads = q_ref.shape[1] // HD
    pieces = []
    for head in range(heads):
        cols = slice(head * HD, (head + 1) * HD)
        scores = dot_nt(k_ref[:, cols], q_ref[:, cols])
        top = jnp.max(scores, 0, keepdims=True)
        weights = jnp.exp(scores - top)
        total = jnp.sum(weights, 0, keepdims=True)
        probs = (weights * (1.0 / total)).astype(BF16)
        pieces.append(dot_tn(v_ref[:, cols], probs))
        log_ref[head : head + 1, :] = top + jnp.log(total)
    mixed_ref[...] = jnp.transpose(jnp.concatenate(pieces, 0)).astype(BF16)


def attend(queries, keys, values):
    capacity, width = queries.shape
    block = 256
    return pl.pallas_call(
        attend_kernel,
        grid=(capacity // block,),
        in_specs=[
            pl.BlockSpec((block, width), lambda b: (b, 0)),
            full((CTX, width)),
            full((CTX, width)),
        ],
        out_specs=[
            pl.BlockSpec((block, width), lambda b: (b, 0)),
            pl.BlockSpec((8, block), lambda b: (0, b)),
        ],
        out_shape=[
            jax.ShapeDtypeStruct((capacity, width), BF16),
            jax.ShapeDtypeStruct((8, capacity), F32),
        ],
        compiler_params=params(),
        cost_estimate=cost(8 * capacity * CTX * width, 3e6),
        name="attend",
    )(queries, keys, values)


def middle_kernel(
    count_ref,
    mixed_ref,
    rows_ref,
    stats_ref,
    w_emb_ref,
    b_emb_ref,
    gain_ref,
    bias_ref,
    out_grad_ref,
    w_out_ref,
    w_fc1_ref,
    b_fc1_ref,
    w_fc2_ref,
    layer_ref,
    mid_ref,
    mixed_grad_ref,
    g_fc1_ref,
    g_b_ref,
    g_fc2_ref,
    g_out_ref,
    g_norm_ref,
    residual_ref,
    normed_ref,
    top_ref,
    final_ref,
    back_ref,
):
    step = pl.program_id(0)
    parts, share, _ = mixed_ref.shape
    valid = lax.broadcasted_iota(jnp.int32, (share, 1), 0) < count_ref[0]

    @pl.when(step == 0)
    def _():
        standard = standardize(rows_ref[...], stats_ref)
        total = dot(standard, w_emb_ref[...]) + b_emb_ref[...]
        for part in range(parts):
            total = total + dot(mixed_ref[part], w_out_ref[part])
        residual_ref[...] = total
        normed_ref[...] = (centre_norm(total)[0] * gain_ref[...] + bias_ref[...]).astype(BF16)
        top_ref[...] = jnp.where(valid, out_grad_ref[...], jnp.zeros_like(out_grad_ref))
        final_ref[...] = jnp.zeros_like(final_ref)
        back_ref[...] = jnp.zeros_like(back_ref)

    pre = dot(normed_ref[...], w_fc1_ref[0]) + b_fc1_ref[0]
    half = 0.5 + 0.5 * lax.erf(pre * 0.7071067811865476)
    activated = (pre * half).astype(BF16)
    slope = half + pre * (0.3989422804014327 * jnp.exp(-0.5 * pre * pre))
    final_ref[...] += dot(activated, w_fc2_ref[0])
    g_fc2_ref[0] = dot_tn(activated, top_ref[...]).astype(BF16)
    pre_grad = (dot_nt(top_ref[...], w_fc2_ref[0]) * slope).astype(BF16)
    g_b_ref[0] = jnp.broadcast_to(
        jnp.sum(pre_grad.astype(F32), 0, keepdims=True), g_b_ref.shape[1:]
    )
    g_fc1_ref[0] = dot_tn(normed_ref[...], pre_grad).astype(BF16)
    back_ref[...] += dot_nt(pre_grad, w_fc1_ref[0])

    @pl.when(step == pl.num_programs(0) - 1)
    def _():
        residual = residual_ref[...]
        layer_ref[...] = jnp.where(valid, residual + final_ref[...], 0.0).astype(BF16)
        unit, rstd = centre_norm(residual)
        grad = back_ref[...]
        g_norm_ref[...] = jnp.zeros_like(g_norm_ref)
        g_norm_ref[0:1, :] = jnp.sum(grad * unit, 0, keepdims=True)
        g_norm_ref[1:2, :] = jnp.sum(grad, 0, keepdims=True)
        scaled = grad * gain_ref[...]
        mid = top_ref[...].astype(F32) + rstd * (
            scaled
            - jnp.mean(scaled, -1, keepdims=True)
            - unit * jnp.mean(scaled * unit, -1, keepdims=True)
        )
        mid_ref[...] = mid
        mid_low = mid.astype(BF16)
        for part in range(parts):
            g_out_ref[part] = dot_tn(mixed_ref[part], mid_low).astype(BF16)
            mixed_grad_ref[part] = dot_nt(mid_low, w_out_ref[part]).astype(BF16)


def middle(count, mixed, rows, stats, w_emb, b_emb, gain, bias, out_grad, w_out, w_fc1, b_fc1, w_fc2):
    parts, share, width = mixed.shape
    model, hidden = w_fc1.shape[1:]
    chunk = lambda s: (s, 0, 0)
    return pl.pallas_call(
        middle_kernel,
        grid=(parts,),
        in_specs=[
            pl.BlockSpec(memory_space=pltpu.SMEM),
            full((parts, share, width)),
            full((share, LANES)),
            full((8, LANES)),
            full((LANES, model)),
            full((1, model)),
            full((1, model)),
            full((1, model)),
            full((share, model)),
            full((parts, width, model)),
            pl.BlockSpec((1, model, hidden), chunk),
            pl.BlockSpec((1, 1, hidden), chunk),
            pl.BlockSpec((1, hidden, model), chunk),
        ],
        out_specs=[
            full((share, model)),
            full((share, model)),
            full((parts, share, width)),
            pl.BlockSpec((1, model, hidden), chunk),
            pl.BlockSpec((1, 8, hidden), chunk),
            pl.BlockSpec((1, hidden, model), chunk),
            full((parts, width, model)),
            full((8, model)),
        ],
        out_shape=[
            jax.ShapeDtypeStruct((share, model), BF16),
            jax.ShapeDtypeStruct((share, model), F32),
            jax.ShapeDtypeStruct((parts, share, width), BF16),
            jax.ShapeDtypeStruct((parts, model, hidden), BF16),
            jax.ShapeDtypeStruct((parts, 8, hidden), F32),
            jax.ShapeDtypeStruct((parts, hidden, model), BF16),
            jax.ShapeDtypeStruct((parts, width, model), BF16),
            jax.ShapeDtypeStruct((8, model), F32),
        ],
        scratch_shapes=[
            pltpu.VMEM((share, model), F32),
            pltpu.VMEM((share, model), BF16),
            pltpu.VMEM((share, model), BF16),
            pltpu.VMEM((share, model), F32),
            pltpu.VMEM((share, model), F32),
        ],
        compiler_params=params(),
        cost_estimate=cost(12 * share * model * hidden * parts * 1.3, 4e7),
        name="middle",
    )(count, mixed, rows, stats, w_emb, b_emb, gain, bias, out_grad, w_out, w_fc1, b_fc1, w_fc2)


def attend_back_kernel(
    q_ref, g_ref, log_ref, k_ref, v_ref, dq_ref, dk_ref, dv_ref, key_total, value_total
):
    step = pl.program_id(0)
    heads = q_ref.shape[1] // HD

    @pl.when(step == 0)
    def _():
        key_total[...] = jnp.zeros_like(key_total)
        value_total[...] = jnp.zeros_like(value_total)

    pieces = []
    for head in range(heads):
        cols = slice(head * HD, (head + 1) * HD)
        query, grad = q_ref[:, cols], g_ref[:, cols]
        key, value = k_ref[:, cols], v_ref[:, cols]
        probs = jnp.exp(dot_nt(key, query) - log_ref[head : head + 1, :])
        value_total[head] += dot(probs.astype(BF16), grad)
        probs_grad = dot_nt(value, grad)
        inner = jnp.sum(probs * probs_grad, 0, keepdims=True)
        score_grad = (probs * (probs_grad - inner)).astype(BF16)
        key_total[head] += dot(score_grad, query)
        pieces.append(dot_tn(key, score_grad))
    dq_ref[...] = (jnp.transpose(jnp.concatenate(pieces, 0)) * SCALE).astype(BF16)

    @pl.when(step == pl.num_programs(0) - 1)
    def _():
        for head in range(heads):
            cols = slice(head * HD, (head + 1) * HD)
            dk_ref[:, cols] = key_total[head].astype(BF16)
            dv_ref[:, cols] = value_total[head].astype(BF16)


def attend_back(queries, grads, logs, keys, values):
    capacity, width = queries.shape
    block = 256
    heads = width // HD
    return pl.pallas_call(
        attend_back_kernel,
        grid=(capacity // block,),
        in_specs=[
            pl.BlockSpec((block, width), lambda b: (b, 0)),
            pl.BlockSpec((block, width), lambda b: (b, 0)),
            pl.BlockSpec((8, block), lambda b: (0, b)),
            full((CTX, width)),
            full((CTX, width)),
        ],
        out_specs=[
            pl.BlockSpec((block, width), lambda b: (b, 0)),
            full((CTX, width)),
            full((CTX, width)),
        ],
        out_shape=[
            jax.ShapeDtypeStruct((capacity, width), BF16),
            jax.ShapeDtypeStruct((CTX, width), BF16),
            jax.ShapeDtypeStruct((CTX, width), BF16),
        ],
        scratch_shapes=[pltpu.VMEM((heads, CTX, HD), F32)] * 2,
        compiler_params=params(),
        cost_estimate=cost(20 * capacity * CTX * width, 4e6),
        name="attend_back",
    )(queries, grads, logs, keys, values)


def finish_kernel(
    block,
    place_ref,
    rows_ref,
    stats_ref,
    w_emb_ref,
    b_emb_ref,
    gain_ref,
    bias_ref,
    w_ref,
    dq_ref,
    dk_ref,
    dv_ref,
    mid_ref,
    g_w_ref,
    g_emb_ref,
    g_small_ref,
    raw_ref,
    w_total,
    back_ref,
    sums_ref,
):
    step = pl.program_id(0)
    last = pl.num_programs(0) - 1
    share = mid_ref.shape[0]
    start = pl.multiple_of(step * block, block)

    @pl.when(step == 0)
    def _():
        w_total[...] = jnp.zeros_like(w_total)
        g_emb_ref[...] = jnp.zeros_like(g_emb_ref)
        g_small_ref[...] = jnp.zeros_like(g_small_ref)
        sums_ref[...] = jnp.zeros_like(sums_ref)

    rows = rows_ref[pl.ds(start, block), :]
    standard = standardize(rows, stats_ref)
    embedded = dot(standard, w_emb_ref[...]) + b_emb_ref[...]
    unit, rstd = centre_norm(embedded)
    normed = (unit * gain_ref[...] + bias_ref[...]).astype(BF16)
    w_total[0] += dot_tn(normed, dq_ref[...])
    back_ref[...] = dot_nt(dq_ref[...], w_ref[0])

    @pl.when(step < CTX // block)
    def _():
        w_total[1] += dot_tn(normed, dk_ref[...])
        w_total[2] += dot_tn(normed, dv_ref[...])
        back_ref[...] += dot_nt(dk_ref[...], w_ref[1]) + dot_nt(dv_ref[...], w_ref[2])

    grad = back_ref[...]
    g_small_ref[0:1, :] += jnp.sum(grad * unit, 0, keepdims=True)
    g_small_ref[1:2, :] += jnp.sum(grad, 0, keepdims=True)
    scaled = grad * gain_ref[...]
    low = rstd * (
        scaled
        - jnp.mean(scaled, -1, keepdims=True)
        - unit * jnp.mean(scaled * unit, -1, keepdims=True)
    )
    back_ref[...] = low
    offset = start - place_ref[0] * share

    @pl.when((offset >= 0) & (offset < share))
    def _():
        inside = pl.multiple_of(jnp.clip(offset, 0, share - block), block)
        back_ref[...] += mid_ref[pl.ds(inside, block), :]

    low_bf = back_ref[...].astype(BF16)
    g_emb_ref[...] += dot_tn(standard, low_bf)
    g_small_ref[2:3, :] += jnp.sum(low_bf.astype(F32), 0, keepdims=True)
    standard_grad = dot_nt(low_bf, w_emb_ref[...])
    raw_ref[pl.ds(start, block), :] = standard_grad
    sums_ref[0:1, :] += jnp.sum(standard_grad, 0, keepdims=True)
    sums_ref[1:2, :] += jnp.sum(standard_grad * rows.astype(F32), 0, keepdims=True)

    @pl.when(step == last)
    def _():
        g_w_ref[...] = w_total[...].astype(BF16)
        mean, r = stats_ref[0:1, :], stats_ref[1:2, :]
        first, second = sums_ref[0:1, :], sums_ref[1:2, :]
        var_grad = -0.5 * r * r * r * (second - mean * first)
        mean_grad = -r * first - 2.0 * mean * var_grad
        context = rows_ref[0:CTX, :].astype(F32)
        raw_ref[...] = raw_ref[...] * r
        raw_ref[0:CTX, :] += (mean_grad + 2.0 * context * var_grad) / CTX


def finish(place, rows, stats, w_emb, b_emb, gain, bias, w_qkv, dq, dk, dv, mid):
    capacity = rows.shape[0]
    model, width = w_emb.shape[1], w_qkv.shape[2]
    share = mid.shape[0]
    block = 256
    ctx_map = lambda b: (jnp.minimum(b, CTX // block - 1), 0)
    return pl.pallas_call(
        functools.partial(finish_kernel, block),
        grid=(capacity // block,),
        in_specs=[
            pl.BlockSpec(memory_space=pltpu.SMEM),
            full((capacity, LANES)),
            full((8, LANES)),
            full((LANES, model)),
            full((1, model)),
            full((1, model)),
            full((1, model)),
            full((3, model, width)),
            pl.BlockSpec((block, width), lambda b: (b, 0)),
            pl.BlockSpec((block, width), ctx_map),
            pl.BlockSpec((block, width), ctx_map),
            full((share, model)),
        ],
        out_specs=[
            full((3, model, width)),
            full((LANES, model)),
            full((8, model)),
            full((capacity, LANES)),
        ],
        out_shape=[
            jax.ShapeDtypeStruct((3, model, width), BF16),
            jax.ShapeDtypeStruct((LANES, model), F32),
            jax.ShapeDtypeStruct((8, model), F32),
            jax.ShapeDtypeStruct((capacity, LANES), F32),
        ],
        scratch_shapes=[
            pltpu.VMEM((3, model, width), F32),
            pltpu.VMEM((block, model), F32),
            pltpu.VMEM((8, LANES), F32),
        ],
        compiler_params=params(),
        cost_estimate=cost(2 * capacity * model * (3 * LANES + 4 * width), 8e6),
        name="finish",
    )(place, rows, stats, w_emb, b_emb, gain, bias, w_qkv, dq, dk, dv, mid)


def shards(
    raw_features,
    placement,
    query_counts,
    out_grad,
    w_emb,
    b_emb,
    ln1_gain,
    ln1_bias,
    w_qkv,
    w_out,
    ln2_gain,
    ln2_bias,
    w_fc1,
    b_fc1,
    w_fc2,
):
    wide, parts = lax.axis_size("wide"), lax.axis_size("narrow")
    wide_index, narrow_index = lax.axis_index("wide"), lax.axis_index("narrow")
    share = out_grad.shape[1]
    capacity = share * parts
    slots = capacity // wide
    features = w_emb.shape[0]
    pad = LANES - features
    row = lambda vector: vector.reshape(1, -1)

    w_out_all = lax.all_gather(w_out, "narrow")
    w_fc1_all = lax.all_gather(w_fc1, "narrow")
    b_fc1_all = lax.all_gather(row(b_fc1), "narrow")
    w_fc2_all = lax.all_gather(w_fc2, "narrow")

    starts = (
        jnp.arange(wide, dtype=jnp.int32) * CTX + jnp.cumsum(query_counts) - query_counts
    ).astype(jnp.int32)
    table = jnp.sum((placement[:, None] >= starts[None, :]).astype(jnp.int32), 1) - 1
    member = table[:, None] == jnp.arange(wide, dtype=jnp.int32)[None, :]
    local = placement - jnp.sum(jnp.where(member, starts[None, :], 0), 1)
    slot = local // wide
    dest = table * slots + slot
    places = jnp.arange(wide * slots, dtype=jnp.int32)
    send_hot = (places[:, None] == dest[None, :]).astype(BF16)
    raw_padded = jnp.pad(raw_features, ((0, 0), (0, pad)))
    outgoing = dot(send_hot, raw_padded).astype(BF16)
    received = lax.all_to_all(outgoing.reshape(wide, slots, LANES), "wide", 0, 0, tiled=True)
    shift = jnp.remainder(starts[wide_index], wide)
    rows = jnp.transpose(jnp.roll(received, -shift, axis=0), (1, 0, 2)).reshape(capacity, LANES)

    w_emb_padded = jnp.pad(w_emb, ((0, pad), (0, 0)))
    embed = (w_emb_padded, row(b_emb))
    norm_one = (row(ln1_gain), row(ln1_bias))
    queries, keys, values, stats = project(rows, *embed, *norm_one, w_qkv)
    mixed, logs = attend(queries, keys, values)
    mixed_share = lax.all_to_all(mixed.reshape(parts, share, -1), "narrow", 0, 0, tiled=True)

    count = (CTX + query_counts[wide_index] - narrow_index * share).reshape(1)
    rows_share = lax.dynamic_slice_in_dim(rows, narrow_index * share, share, 0)
    layer_out, mid, mixed_grad, g_fc1, g_b_fc1, g_fc2, g_out, g_norm = middle(
        count,
        mixed_share,
        rows_share,
        stats,
        *embed,
        row(ln2_gain),
        row(ln2_bias),
        out_grad[0],
        w_out_all,
        w_fc1_all,
        b_fc1_all,
        w_fc2_all,
    )
    g_fc1, g_fc2, g_out, g_b_fc1 = [
        lax.psum_scatter(term, "narrow", scatter_dimension=0)
        for term in (g_fc1, g_fc2, g_out, g_b_fc1)
    ]
    grads = lax.all_to_all(mixed_grad, "narrow", 0, 0, tiled=True).reshape(capacity, -1)
    dq, dk, dv = attend_back(queries, grads, logs, keys, values)
    g_qkv, g_emb, g_small, raw_rows = finish(
        narrow_index.reshape(1), rows, stats, *embed, *norm_one, w_qkv, dq, dk, dv, mid
    )

    raw_parts = lax.all_to_all(
        raw_rows.astype(BF16).reshape(parts, share, LANES), "narrow", 0, 0, tiled=True
    )
    raw_share = jnp.sum(raw_parts.astype(F32), 0).astype(BF16)
    split = jnp.transpose(raw_share.reshape(share // wide, wide, LANES), (1, 0, 2))
    returned = lax.all_to_all(jnp.roll(split, shift, axis=0), "wide", 0, 0, tiled=True)
    gathered = lax.all_gather(returned, "narrow").reshape(-1, LANES)
    piece = slots // parts
    back = (slot // piece) * (wide * piece) + table * piece + slot % piece
    back_hot = (back[:, None] == places[None, :]).astype(BF16)
    raw_grad = dot(back_hot, gathered)[:, :features]

    small = jnp.concatenate([g_emb, g_small, g_norm], 0)
    small = lax.psum(small, ("wide", "narrow"))
    g_qkv, g_fc1, g_fc2, g_out, g_b_fc1 = lax.psum((g_qkv, g_fc1, g_fc2, g_out, g_b_fc1), "wide")
    return (
        layer_out[None],
        raw_grad,
        small[:features],
        small[LANES + 2],
        small[LANES],
        small[LANES + 1],
        g_qkv.astype(F32),
        g_out.astype(F32),
        small[LANES + 8],
        small[LANES + 9],
        g_fc1.astype(F32),
        g_b_fc1[0],
        g_fc2.astype(F32),
    )


def solution(mesh):
    in_specs = (
        P("wide", None),
        P("wide"),
        P(),
        P("wide", "narrow", None),
        P(),
        P(),
        P(),
        P(),
        P(None, None, "narrow"),
        P("narrow", None),
        P(),
        P(),
        P(None, "narrow"),
        P("narrow"),
        P("narrow", None),
    )
    out_specs = (
        P("wide", "narrow", None),
        P("wide", None),
        P(),
        P(),
        P(),
        P(),
        P(None, None, "narrow"),
        P("narrow", None),
        P(),
        P(),
        P(None, "narrow"),
        P("narrow"),
        P("narrow", None),
    )
    return jax.shard_map(shards, mesh=mesh, in_specs=in_specs, out_specs=out_specs, check_vma=False)
```

time: 1040 us -> 585 us (0.56); the launches traced: 1030 us -> 585 us
  waiting for transfers between devices: 650 us -> 339 us
  matrix products: 116 us -> 5.9 us
  Pallas kernels: 0 us -> 108 us
  other arithmetic: 58.8 us -> 7.44 us
  blocking collectives: 105 us -> 60.9 us
  local copies, waits for them, and re-layouts: 66.8 us -> 22.8 us
  starting transfers between devices: 11.5 us -> 24 us
    all_to_all x2 -> x5, waiting for transfers between devices: 184 us -> 29.7 us  [the longest x1 12.9 us: shards(): lax.all_to_all(mixed_grad, 'narrow', 0, 0, tiled=True).reshape(capacity, -1)]
    reduce_scatter x4, waiting for transfers between devices: 205 us -> 54.4 us  [shards(): lax.psum_scatter(term, 'narrow', scatter_dimension=0)]
    dot_general x57 -> x2, matrix products: 116 us -> 5.9 us  [dot(): return jnp.dot(left, right, preferred_element_type=F32)]
    pallas_call x0 -> x5, Pallas kernels: none -> 108 us  [the longest x1 29.4 us: attend_back(): pl.pallas_call(attend_back_kernel, grid=(capacity // block,), in_specs=[p...]
    all_gather x4 -> x3, waiting for transfers between devices: 104 us -> 17.4 us  [the longest x1 17.4 us: shards(): w_fc2_all = lax.all_gather(w_fc2, 'narrow')]
    psum x1 -> x2, waiting for transfers between devices: 157 us -> 233 us  [the longest x1 138 us: shards(): lax.psum((g_qkv, g_fc1, g_fc2, g_out, g_b_fc1), 'wide')]
    psum x3 -> x1, blocking collectives: 105 us -> 37.8 us  [shards(): lax.psum((g_qkv, g_fc1, g_fc2, g_out, g_b_fc1), 'wide')]
    reduce_sum x16 -> x3, other arithmetic: 32.5 us -> 0.25 us  [the longest x1 0.09 us: shards(): jnp.sum((placement[:, None] >= starts[None, :]).astype(jnp.int32), 1) - 1]
  transfers between devices with their start and end apart: 11 -> 14, of which waited for: 11 -> 9; matrix products, arithmetic and copies ran while one was open for 4% -> 5% of each run, Pallas kernels for 0% -> 14%
where the time goes in v1:
time: 585 us
  waiting for transfers between devices  339 us (58%)
  Pallas kernels  108 us (18%)
  blocking collectives  60.9 us (10%)
  starting transfers between devices  24 us (4%)
  local copies, waits for them, and re-layouts  22.8 us (4%)
  between operations  16.7 us (3%)
  other arithmetic  7.44 us (1%)
  matrix products  5.9 us (1%)
    psum x1, waiting for transfers between devices, shards(): lax.psum((g_qkv, g_fc1, g_fc2, g_out, g_b_fc1), 'wide')  138 us
    psum x1, waiting for transfers between devices, shards(): small = lax.psum(small, ('wide', 'narrow'))  94.8 us
    reduce_scatter x4, waiting for transfers between devices, shards(): lax.psum_scatter(term, 'narrow', scatter_dimension=0)  54.4 us
    psum x1, blocking collectives, shards(): lax.psum((g_qkv, g_fc1, g_fc2, g_out, g_b_fc1), 'wide')  37.8 us
    pallas_call x1, Pallas kernels, attend_back(): pl.pallas_call(attend_back_kernel, grid=(capacity // block,), in_specs=[p...  29.4 us
    pallas_call x1, Pallas kernels, middle(): pl.pallas_call(middle_kernel, grid=(parts,), in_specs=[pl.BlockSpec(memor...  26.7 us
    pallas_call x1, Pallas kernels, attend(): pl.pallas_call(attend_kernel, grid=(capacity // block,), in_specs=[pl.Blo...  22.5 us
    pallas_call x1, Pallas kernels, finish(): pl.pallas_call(functools.partial(finish_kernel, block), grid=(capacity //...  19.7 us
  transfers between devices with their start and end apart: 14, of which 9 were waited for; matrix products, arithmetic and copies ran while one was open for 5% of the time, Pallas kernels for 14%

profile of v1, /device:TPU:0, one launch (start us, length us, event | category | flops | bytes accessed | tf_op | source)
XLA Modules:
  0.0 584.5 jit_solution(6160080463696401323)
XLA Ops:
  9.9 2.7 fusion.4
  12.6 7.4 %all-to-all-start = ((bf16[8,256,128]{2,1,0:T(8,128)(2,1)}), bf16[8,256,128]{2,1,0:T(8,128)(2,1)S(1)}, u32[]{:S(2)}, u32[]{:S(2)}) async-start(bf16[8,256,128]{2,1,0:T(8,128)(2,1)} %bitcast.4), calls=%async_computation | async-start | bytes 1048576 | tf_op jit(solution)/shard_map/all_to_all | solution.py:525
  26.4 8.1 %all-to-all-done = bf16[8,256,128]{2,1,0:T(8,128)(2,1)S(1)} async-done(((bf16[8,256,128]{2,1,0:T(8,128)(2,1)}), bf16[8,256,128]{2,1,0:T(8,128)(2,1)S(1)}, u32[]{:S(2)}, u32[]{:S(2)}) %all-to-all-start) | async-done | bytes 524320 | tf_op jit(solution)/shard_map/all_to_all | solution.py:525
  35.8 10.1 %project.1 = (bf16[2048,192]{1,0:T(8,128)(2,1)}, bf16[1024,192]{1,0:T(8,128)(2,1)}, bf16[1024,192]{1,0:T(8,128)(2,1)}, f32[8,128]{1,0:T(8,128)}) custom-call(bf16[2048,128]{1,0:T(8,128)(2,1)} %bitcast.35, bf16[128,768]{1,0:T(8,128)(2,1)} %pad.9.w_emb_ref, f32[1,768]{1,0:T(1,128)} %reshape.108.b_emb_ref, f32[1,768]{1,0:T(1,128)} %reshape.109.gain_ref, ...), custom_call_target="tpu_custom_call" | custom-call | flops 1610612736 | bytes 4000000 | tf_op jit(solution)/shard_map/project/pallas_call | solution.py:84
  45.9 22.5 %attend.1 = (bf16[2048,192]{1,0:T(8,128)(2,1)}, f32[8,2048]{1,0:T(8,128)}) custom-call(bf16[2048,192]{1,0:T(8,128)(2,1)} %get-tuple-element.34.q_ref, bf16[1024,192]{1,0:T(8,128)(2,1)} %get-tuple-element.35.k_ref, bf16[1024,192]{1,0:T(8,128)(2,1)} %get-tuple-element.36.v_ref), custom_call_target="tpu_custom_call" | custom-call | flops 3221225472 | bytes 3000000 | tf_op jit(solution)/shard_map/attend/pallas_call | solution.py:131
  70.6 3.5 all-to-all-start.1
  76.6 15.8 %all-gather.5.b_fc1_ref = f32[4,1,768]{2,1,0:T(1,128)} all-gather(f32[1,1,768]{2,1,0:T(1,128)S(1)} %reshape.125), channel_id=4, replica_groups=mesh['wide'=8,'narrow'=4] {'narrow'}, dimensions={0}, use_global_device_ids=true | all-gather | bytes 15360 | tf_op jit(solution)/shard_map/all_gather | solution.py:510
  95.3 17.4 %all-gather.14.cloned.1.call-done = bf16[3072,768]{1,0:T(8,128)(2,1)} async-done(((bf16[768,768]{1,0:T(8,128)(2,1)}), bf16[3072,768]{1,0:T(8,128)(2,1)}) %all-gather.14.cloned.1.call-update) | async-done | bytes 4718608 | tf_op jit(solution)/shard_map/all_gather | solution.py:511
  112.7 26.7 %middle.1 = (bf16[512,768]{1,0:T(8,128)(2,1)}, f32[512,768]{1,0:T(8,128)}, bf16[4,512,192]{2,1,0:T(8,128)(2,1)}, bf16[4,768,768]{2,1,0:T(8,128)(2,1)}, f32[4,8,7...) custom-call(s32[1]{0:T(128)} %bitcast.1.count_ref, ...), custom_call_target="tpu_custom_call" | custom-call | flops 18844168192 | bytes 40000000 | tf_op jit(solution)/shard_map/middle/pallas_call | solution.py:236
  142.5 3.5 all-to-all-start.2
  147.0 12.9 %all-to-all-done.2 = bf16[4,512,192]{1,2,0:T(8,128)(2,1)S(1)} async-done(((bf16[4,512,192]{1,2,0:T(8,128)(2,1)}), bf16[4,512,192]{1,2,0:T(8,128)(2,1)S(1)}, u32[]{:S(2)}, u32[]{:S(2)}) %all-to-all-start.2) | async-done | bytes 786464 | tf_op jit(solution)/shard_map/all_to_all | solution.py:556
  161.2 29.4 %attend_back.1 = (bf16[2048,192]{1,0:T(8,128)(2,1)}, bf16[1024,192]{1,0:T(8,128)(2,1)}, bf16[1024,192]{1,0:T(8,128)(2,1)}) custom-call(bf16[2048,192]{1,0:T(8,128)(2,1)} %get-tuple-element.34.q_ref, bf16[2048,192]{1,0:T(8,128)(2,1)} %bitcast.33, f32[8,2048]{1,0:T(8,128)} %get-tuple-element.41.log_ref, bf16[1024,192]{1,0:T(8,128)(2,1)} %get-tuple-element.35.k_ref, ...), custom_call_target="tpu_custom_call" | custom-call | flops 8053063680 | bytes 4000000 | tf_op jit(solution)/shard_map/attend_back/pallas_call | solution.py:324
  190.6 19.7 %finish.1 = (bf16[3,768,192]{2,1,0:T(8,128)(2,1)}, f32[128,768]{1,0:T(8,128)}, f32[8,768]{1,0:T(8,128)}, f32[2048,128]{1,0:T(8,128)}) custom-call(s32[1]{0:T(128)} %bitcast.14.place_ref, bf16[2048,128]{1,0:T(8,128)(2,1)} %bitcast.37, f32[8,128]{1,0:T(8,128)} %get-tuple-element.38.stats_ref, bf16[128,768]{1,0:T(8,128)(2,1)} %pad.9.w_emb_ref, ...), custom_call_target="tpu_custom_call" | custom-call | flops 3623878656 | bytes 8000000 | tf_op jit(solution)/shard_map/finish/pallas_call | solution.py:442
  213.6 50.4 %reduce-scatter.11.cloned.1.call-done = bf16[1,768,768]{2,1,0:T(8,128)(2,1)} async-done(((bf16[4,768,768]{2,1,0:T(8,128)(2,1)}), bf16[1,768,768]{2,1,0:T(8,128)(2,1)}) %reduce-scatter.11.cloned.1.call-update) | async-done | bytes 1179664 | tf_op jit(solution)/shard_map/reduce_scatter | solution.py:553
  264.9 3.5 all-to-all-start.3
  268.4 8.8 %all-to-all-done.3 = bf16[4,512,128]{2,1,0:T(8,128)(2,1)S(1)} async-done(((bf16[4,512,128]{2,1,0:T(8,128)(2,1)}), bf16[4,512,128]{2,1,0:T(8,128)(2,1)S(1)}, u32[]{:S(2)}, u32[]{:S(2)}) %all-to-all-start.3) | async-done | bytes 524320 | tf_op jit(solution)/shard_map/all_to_all | solution.py:562
  278.0 5.5 all-to-all-start.4
  283.5 2.5 reduce-scatter.9.cloned.1.call-done
  286.1 37.8 %psum.46 = f32[8,768]{1,0:T(8,128)S(1)} all-reduce(f32[8,768]{1,0:T(8,128)} %bitcast.41), channel_id=1, replica_groups=mesh['wide'=8,'narrow'=4] {'wide'}, use_global_device_ids=true, to_apply=%region_11.12 | all-reduce | flops 6144 | bytes 49152 | tf_op jit(solution)/shard_map/psum | solution.py:576
  324.5 94.8 %all-reduce.6.cloned.1.call-done = f32[144,768]{1,0:T(8,128)} async-done(((f32[144,768]{1,0:T(8,128)}), f32[144,768]{1,0:T(8,128)}) %all-reduce.6.cloned.1.call-update) | async-done | bytes 442384 | tf_op jit(solution)/shard_map/psum | solution.py:575
  422.5 7.2 %all-gather.4 = bf16[32,64,128]{2,1,0:T(8,128)(2,1)S(1)} all-gather(bf16[8,64,128]{2,1,0:T(8,128)(2,1)S(1)} %all-to-all-done.4), channel_id=6, replica_groups=mesh['wide'=8,'narrow'=4] {'narrow'}, dimensions={0}, use_global_device_ids=true | all-gather | bytes 655360 | tf_op jit(solution)/shard_map/all_gather | solution.py:568
  429.7 3.2 fusion.1
  432.9 138.4 %all-reduce.8.cloned.1.call-done = (bf16[3,768,192]{2,1,0:T(8,128)(2,1)}, bf16[192,768]{1,0:T(8,128)(2,1)}, bf16[768,768]{1,0:T(8,128)(2,1)}, bf16[768,768]{1,0:T(8,128)(2,1)}) async-done(((bf16[3,768,192]{2,1,0:T(8,128)(2,1)}, bf16[192,768]{1,0:T(8,128)(2,1)}, bf16[768,768]{1,0:T(8,128)(2,1)}, bf16[768,768]{1,0:T(8,128)(2,1)}), (bf16[3,768,192]{2,1,0:T(8,128)(2,1)}, bf16[192,768]{1,0:T(8,128)(2,1)}, ...) | async-done | bytes 3538960 | tf_op jit(solution)/shard_map/psum | solution.py:576
  571.4 2.6 copy.67
  (92 shorter events, 33.6 us)
Async XLA Ops:
  7.2 88.0 %all-gather.10.cloned.1.call-start = ((), (), s32[]{:S(2)}) async-start(), calls=%async_computation.14 | async-start | bytes 1474560 | tf_op jit(solution)/shard_map/all_gather | solution.py:508
  7.9 87.3 %all-gather.12.cloned.1.call-start = ((), (), s32[]{:S(2)}) async-start(), calls=%async_computation.15 | async-start | bytes 5898240 | tf_op jit(solution)/shard_map/all_gather | solution.py:509
  8.7 104.0 %all-gather.14.cloned.1.call-start = ((), (), s32[]{:S(2)}) async-start(), calls=%async_computation.16 | async-start | bytes 5898240 | tf_op jit(solution)/shard_map/all_gather | solution.py:511
  9.9 12.7 %copy-start.9 = (f32[768]{0:T(1024)S(1)}, f32[768]{0:T(1024)}, u32[]{:S(2)}) copy-start(f32[768]{0:T(1024)} %param.20) | copy-start | bytes 9220
  9.9 13.3 %copy-start.10 = (f32[768]{0:T(1024)S(1)}, f32[768]{0:T(1024)}, u32[]{:S(2)}) copy-start(f32[768]{0:T(1024)} %param.21) | copy-start | bytes 9220
  9.9 13.9 %copy-start.11 = (f32[768]{0:T(1024)S(1)}, f32[768]{0:T(1024)}, u32[]{:S(2)}) copy-start(f32[768]{0:T(1024)} %param.22) | copy-start | bytes 9220
  9.9 14.4 %copy-start.4 = (bf16[3,768,192]{1,2,0:T(8,128)(2,1)S(1)}, bf16[3,768,192]{1,2,0:T(8,128)(2,1)}, u32[]{:S(2)}) copy-start(bf16[3,768,192]{1,2,0:T(8,128)(2,1)} %param.23) | copy-start | bytes 2654212
  12.6 13.1 %copy-start.6 = (bf16[100,768]{1,0:T(8,128)(2,1)S(1)}, bf16[100,768]{1,0:T(8,128)(2,1)}, u32[]{:S(2)}) copy-start(bf16[100,768]{1,0:T(8,128)(2,1)} %param.19) | copy-start | bytes 460804
  12.6 21.9 %all-to-all-start = ((bf16[8,256,128]{2,1,0:T(8,128)(2,1)}), bf16[8,256,128]{2,1,0:T(8,128)(2,1)S(1)}, u32[]{:S(2)}, u32[]{:S(2)}) async-start(bf16[8,256,128]{2,1,0:T(8,128)(2,1)} %bitcast.4), calls=%async_computation | async-start | bytes 1048576 | tf_op jit(solution)/shard_map/all_to_all | solution.py:525
  68.4 7.0 %copy-start.12 = (f32[768]{0:T(1024)S(1)}, f32[768]{0:T(1024)}, u32[]{:S(2)}) copy-start(f32[768]{0:T(1024)} %param.25) | copy-start | bytes 9220
  68.4 7.6 %copy-start.13 = (f32[768]{0:T(1024)S(1)}, f32[768]{0:T(1024)}, u32[]{:S(2)}) copy-start(f32[768]{0:T(1024)} %param.26) | copy-start | bytes 9220
  68.4 8.2 %copy-start.14 = (f32[768]{0:T(1024)S(1)}, f32[768]{0:T(1024)}, u32[]{:S(2)}) copy-start(f32[768]{0:T(1024)} %param.28) | copy-start | bytes 9220
  70.6 23.4 %all-to-all-start.1 = ((bf16[4,512,192]{1,2,0:T(8,128)(2,1)}), bf16[4,512,192]{1,2,0:T(8,128)(2,1)S(1)}, u32[]{:S(2)}, u32[]{:S(2)}) async-start(bf16[4,512,192]{1,2,0:T(8,128)(2,1)} %copy.61), calls=%async_computation.1 | async-start | bytes 1572864 | tf_op jit(solution)/shard_map/all_to_all | solution.py:534
  74.1 138.0 %reduce-scatter.5.cloned.1.call-start = ((), (), s32[]{:S(2)}) async-start(), calls=%async_computation.10 | async-start | bytes 1474560 | tf_op jit(solution)/shard_map/reduce_scatter | solution.py:553
  139.4 74.3 %reduce-scatter.7.cloned.1.call-start = ((), (), s32[]{:S(2)}) async-start(), calls=%async_computation.11 | async-start | bytes 5898240 | tf_op jit(solution)/shard_map/reduce_scatter | solution.py:553
  140.0 124.1 %reduce-scatter.11.cloned.1.call-start = ((), (), s32[]{:S(2)}) async-start(), calls=%async_computation.13 | async-start | bytes 5898240 | tf_op jit(solution)/shard_map/reduce_scatter | solution.py:553
  142.5 17.4 %all-to-all-start.2 = ((bf16[4,512,192]{1,2,0:T(8,128)(2,1)}), bf16[4,512,192]{1,2,0:T(8,128)(2,1)S(1)}, u32[]{:S(2)}, u32[]{:S(2)}) async-start(bf16[4,512,192]{1,2,0:T(8,128)(2,1)} %copy.63), calls=%async_computation.2 | async-start | bytes 1572864 | tf_op jit(solution)/shard_map/all_to_all | solution.py:556
  146.0 140.1 %reduce-scatter.9.cloned.1.call-start = ((), (), s32[]{:S(2)}) async-start(), calls=%async_computation.12 | async-start | bytes 122880 | tf_op jit(solution)/shard_map/reduce_scatter | solution.py:553
  146.7 272.5 %all-reduce.6.cloned.1.call-start = ((), (), s32[]{:S(2)}) async-start(), calls=%async_computation.9 | async-start | bytes 884736 | tf_op jit(solution)/shard_map/psum | solution.py:575
  190.6 19.7 %copy-start.8 = (f32[8,768]{1,0:T(8,128)S(1)}, f32[8,768]{1,0:T(8,128)}, u32[]{:S(2)}) copy-start(f32[8,768]{1,0:T(8,128)} %get-tuple-element.49) | copy-start | bytes 73732
  212.0 52.0 %copy-start.3 = (f32[2048,128]{1,0:T(8,128)S(1)}, f32[2048,128]{1,0:T(8,128)}, u32[]{:S(2)}) copy-start(f32[2048,128]{1,0:T(8,128)} %get-tuple-element.46) | copy-start | bytes 3145732
  212.1 359.3 %all-reduce.8.cloned.1.call-start = ((), (), s32[]{:S(2)}) async-start(), calls=%async_computation.17 | async-start | bytes 7667712 | tf_op jit(solution)/shard_map/psum | solution.py:576
  264.9 12.3 %all-to-all-start.3 = ((bf16[4,512,128]{2,1,0:T(8,128)(2,1)}), bf16[4,512,128]{2,1,0:T(8,128)(2,1)S(1)}, u32[]{:S(2)}, u32[]{:S(2)}) async-start(bf16[4,512,128]{2,1,0:T(8,128)(2,1)} %bitcast.16), calls=%async_computation.3 | async-start | bytes 1048576 | tf_op jit(solution)/shard_map/all_to_all | solution.py:562
  278.0 144.4 %all-to-all-start.4 = ((bf16[8,64,128]{2,1,0:T(8,128)(2,1)}), bf16[8,64,128]{2,1,0:T(8,128)(2,1)S(1)}, u32[]{:S(2)}, u32[]{:S(2)}) async-start(bf16[8,64,128]{2,1,0:T(8,128)(2,1)} %copy.66), calls=%async_computation.4 | async-start | bytes 262144 | tf_op jit(solution)/shard_map/all_to_all | solution.py:567
  (7 other events, 17.1 us)
Sparse Core Ops, SparseCore 0:
  9.6 20.1 all-gather.9
  31.4 37.4 all-gather.11
  70.4 42.2 all-gather.13
  139.5 25.4 reduce-scatter.4
  167.4 46.1 reduce-scatter.6
  216.0 47.9 reduce-scatter.10
  266.4 19.5 reduce-scatter.8
  291.9 127.2 all-reduce.5
  423.3 148.0 all-reduce.7
